TPU v7x, 32 devices: a whole 2x2x4 slice. The times are simulated.
32 devices in a mesh: groups: 2 (over y), seg: 4 (over z), bin: 4 (over x, core).
Axes of the slice: x: 2, y: 2, z: 4, core: 2. Of those that a mesh axis runs over, the one named last changes fastest.
Arguments:
- start_factors: float32 [4096, 128], P(('groups', 'seg', 'bin')), parts along dimension 0, may hold values from -6 to 6
- bin_factors: bfloat16 [8192, 128], P(('groups', 'bin')), parts along dimension 0, may hold values from -0.5 to 0.5
- tile_speed: bfloat16 [8, 4, 12, 128, 128], P(('groups', 'seg'), 'bin'), parts along dimension 0, may hold values from -6 to 6
- tile_weight: bfloat16 [8, 4, 12, 128, 128], P(('groups', 'seg'), 'bin'), parts along dimension 0, may hold values from 0.099609375 to 2
- tile_cells: int32 [8, 4, 12, 2], P(('groups', 'seg'), 'bin'), parts along dimension 0, may hold values from 0 to 7, as said below
- tile_count: int32 [8, 4], P(('groups', 'seg'), 'bin'), parts along dimension 0, may hold values from 1 to 12, as said below
- inner_pairs: int32 [8, 4, 2, 2], P(('groups', 'seg'), 'bin'), parts along dimension 0, may hold values from 0 to 3, as said below
- inner_weight: float32 [8, 4, 2, 128, 128], P(('groups', 'seg'), 'bin'), parts along dimension 0, may hold values from 0 to 0.00390625
- face_rows: int32 [8, 4, 2, 256], P(('groups', 'seg'), 'bin'), parts along dimension 0, may hold values from 0 to 511, as said below
- face_count: int32 [8, 4, 2], P(('groups', 'seg'), 'bin'), parts along dimension 0, may hold values from 128 to 256, as said below
- face_weight: float32 [8, 4, 256, 256], P(('groups', 'seg'), 'bin'), parts along dimension 0, may hold values from 0 to 0.00390625
Outputs:
- solution_factors: float32 [4096, 128], P(('groups', 'seg', 'bin')), parts along dimension 0
- residual: float32 [4096, 128], P(('groups', 'seg', 'bin')), parts along dimension 0
There are 2 independent parts, one for each index of `groups`. A program takes and returns all parts, laid end to end along the dimension named above; each array names one. Nothing has to cross between parts.
Inputs may be any that keep to these rules, and one draw needn't show every extreme that they name: `tile_cells`: the 12 slots of one device name different pairs; the first entry is a segment block of the partition, the second a bin block of the device's bins. `tile_count`: some device of every draw has all 12 slots live. `inner_pairs`: the two blocks of a pair differ; both are segment blocks of the partition. `face_rows`: row numbers within the partition, different within each face list. `face_count`: some face list of every draw has all 256 rows live.
All inputs are finite; a program needn't handle non-finite values.
Results may differ from a plain program's by a relative error of at most 0.0024.
Values sent between devices are 32-bit elements; how exact they have to be, the bound alone decides.
No kernel may reach another device: no remote copies, remote signals or barrier semaphores. Data moves between devices by JAX's collectives and lax.ppermute only.
A program may use at most 64 MiB of HBM per device.

v0:
```python
import jax
import jax.numpy as jnp
from jax import lax
from jax.sharding import PartitionSpec as P

ITERS = 2
highest = lax.Precision.HIGHEST
ridge_weight = 0.5


def from_behind(x, axis, by):
    devices = lax.axis_size(axis)
    pairs = [(i, i + by) for i in range(devices) if 0 <= i + by < devices]
    return lax.ppermute(x, axis, pairs)


def shards(
    start_factors,
    bin_factors,
    tile_speed,
    tile_weight,
    tile_cells,
    tile_count,
    inner_pairs,
    inner_weight,
    face_rows,
    face_count,
    face_weight,
):
    speeds = tile_speed[0, 0]
    weights = tile_weight[0, 0]
    cells = tile_cells[0, 0]
    n_tiles = speeds.shape[0]
    tile_size = speeds.shape[1]
    own_rows = start_factors.shape[0]
    width = start_factors.shape[1]
    part_rows = own_rows * lax.axis_size("bin")
    part_blocks = part_rows // tile_size
    block_ids = jnp.arange(part_blocks, dtype=jnp.int32)
    live_tiles = (jnp.arange(n_tiles, dtype=jnp.int32) < tile_count[0, 0]).astype(jnp.float32)
    tile_bins = bin_factors.reshape(-1, tile_size, width)[cells[:, 1]]
    bins_wide = tile_bins.astype(jnp.float32)
    tile_gain = weights.astype(jnp.float32) * live_tiles[:, None, None]
    tile_onehot = (cells[:, 0][:, None] == block_ids[None, :]).astype(jnp.float32)
    weighted = (weights.astype(jnp.float32) * speeds.astype(jnp.float32)).astype(jnp.bfloat16)
    rhs_terms = jnp.einsum("kij,kjr->kir", weighted, tile_bins, preferred_element_type=jnp.float32)
    rhs_terms = rhs_terms * live_tiles[:, None, None]
    rhs_part = jnp.einsum("kb,kir->bir", tile_onehot, rhs_terms, precision=highest).reshape(
        part_rows, width
    )
    pairs = inner_pairs[0, 0]
    pair_weight = inner_weight[0, 0]
    left_onehot = (pairs[:, 0][:, None] == block_ids[None, :]).astype(jnp.float32)
    right_onehot = (pairs[:, 1][:, None] == block_ids[None, :]).astype(jnp.float32)
    left_degree = pair_weight.sum(2)
    right_degree = pair_weight.sum(1)
    rows_low = face_rows[0, 0, 0]
    rows_up = face_rows[0, 0, 1]
    face_slots = jnp.arange(rows_low.shape[0], dtype=jnp.int32)
    mask_low = (face_slots < face_count[0, 0, 0]).astype(jnp.float32)
    mask_up = (face_slots < face_count[0, 0, 1]).astype(jnp.float32)
    upper_count = face_count[0, 0, 1:2]
    face_block = face_weight[0, 0]

    def apply_local(whole_rows):
        blocks = whole_rows.reshape(part_blocks, tile_size, width)
        picked = blocks[cells[:, 0]]
        scores = jnp.einsum("kir,kjr->kij", picked, bins_wide, precision=highest) * tile_gain
        pulled = jnp.einsum("kij,kjr->kir", scores, bins_wide, precision=highest)
        left = blocks[pairs[:, 0]]
        right = blocks[pairs[:, 1]]
        to_left = left_degree[..., None] * left - jnp.einsum(
            "kij,kjr->kir", pair_weight, right, precision=highest
        )
        to_right = right_degree[..., None] * right - jnp.einsum(
            "kij,kir->kjr", pair_weight, left, precision=highest
        )
        summed = jnp.einsum("kb,kir->bir", tile_onehot, pulled, precision=highest)
        summed = summed + jnp.einsum("kb,kir->bir", left_onehot, to_left, precision=highest)
        summed = summed + jnp.einsum("kb,kir->bir", right_onehot, to_right, precision=highest)
        summed = summed.reshape(part_rows, width)
        own_face = whole_rows[rows_low] * mask_low[:, None]
        upper_face = whole_rows[rows_up] * mask_up[:, None]
        lower_face, lower_count = from_behind((upper_face, upper_count), "seg", 1)
        lower_mask = (face_slots < lower_count[0]).astype(jnp.float32)
        coupling = face_block * mask_low[:, None] * lower_mask[None, :]
        own_term = coupling.sum(1)[:, None] * own_face - jnp.dot(
            coupling, lower_face, precision=highest
        )
        answer = coupling.sum(0)[:, None] * lower_face - jnp.dot(
            coupling.T, own_face, precision=highest
        )
        returned = from_behind(answer, "seg", -1)
        return summed.at[rows_low].add(own_term).at[rows_up].add(returned)

    def reduce_rows(partial_value):
        reduced = lax.psum_scatter(partial_value, "bin", scatter_dimension=0, tiled=True)
        return reduced

    def spread(vector):
        whole_rows = lax.all_gather(vector, "bin", axis=0, tiled=True)
        return whole_rows

    def fold_sum(values):
        folded = lax.psum((values[0], values[1]), ("seg", "bin"))
        return folded

    def image_of(vector):
        return reduce_rows(apply_local(spread(vector))) + ridge_weight * vector

    start_whole = lax.all_gather(start_factors, "bin", axis=0, tiled=True)
    residual = reduce_rows(rhs_part - apply_local(start_whole)) - ridge_weight * start_factors
    solution = start_factors
    images = image_of(residual)
    norm_now, product = fold_sum((jnp.sum(residual * residual), jnp.sum(residual * images)))
    step_size = norm_now / product
    direction = residual
    along = images
    for iteration in range(ITERS):
        solution = solution + step_size * direction
        residual = residual - step_size * along
        if iteration + 1 < ITERS:
            images = image_of(residual)
            norm_next, product = fold_sum(
                (jnp.sum(residual * residual), jnp.sum(residual * images))
            )
            beta_ratio = norm_next / norm_now
            step_size = norm_next / (product - beta_ratio * norm_next / step_size)
            direction = residual + beta_ratio * direction
            along = images + beta_ratio * along
            norm_now = norm_next
    outputs = (solution, residual)
    return outputs


def solution(mesh):
    return jax.shard_map(
        shards,
        mesh=mesh,
        in_specs=(
            P(("groups", "seg", "bin"), None),
            P(("groups", "bin"), None),
            P(("groups", "seg"), "bin", None, None, None),
            P(("groups", "seg"), "bin", None, None, None),
            P(("groups", "seg"), "bin", None, None),
            P(("groups", "seg"), "bin"),
            P(("groups", "seg"), "bin", None, None),
            P(("groups", "seg"), "bin", None, None, None),
            P(("groups", "seg"), "bin", None, None),
            P(("groups", "seg"), "bin", None),
            P(("groups", "seg"), "bin", None, None),
        ),
        out_specs=(P(("groups", "seg", "bin"), None), P(("groups", "seg", "bin"), None)),
        check_vma=False,
    )
```

profile of v0, /device:TPU:0, one launch (start us, length us, event | category | flops | bytes accessed | tf_op | source)
XLA Modules:
  0.0 242.0 jit_solution(7704379374900717921)
XLA Ops:
  7.2 1.4 fusion.76
  8.6 5.6 %collective-permute-start = (s32[1]{0:T(128)}, s32[1]{0:T(128)}, u32[]{:S(2)}, u32[]{:S(2)}) collective-permute-start(s32[1]{0:T(128)} %bitcast.23), channel_id=1, source_target_pairs={{0,4},{4,8},{8,12},{1,5},{5,9},{9,13},{2,6},{6,10},{10,14},{3,7},{... | collective-permute-start | bytes 20 | tf_op jit(solution)/shard_map/ppermute | solution.py:14
  14.2 6.0 %all_gather.9 = f32[512,128]{1,0:T(8,128)S(1)} all-gather(f32[128,128]{1,0:T(8,128)} %param.11), channel_id=1, replica_groups=mesh['groups'=2,'seg'=4,'bin'=4] {'bin'}, dimensions={0}, use_global_device_ids=true | all-gather | bytes 327680 | tf_op jit(solution)/shard_map/all_gather | solution.py:111
  21.7 3.0 %collective-permute-start.1 = (f32[256,128]{1,0:T(8,128)S(1)}, f32[256,128]{1,0:T(8,128)S(1)}, u32[]{:S(2)}, u32[]{:S(2)}) collective-permute-start(f32[256,128]{1,0:T(8,128)S(1)} %broadcast_multiply_fusion.2), channel_id=1, source_target_pairs={{0,4},{4,8},{8,12},{1,5},{5,9},{9,13},{2,6},{6,10},{10,14},{3,7},{... | collective-permute-start | bytes 393224 | tf_op jit(solution)/shard_map/ppermute | solution.py:14
  40.1 2.0 scatter_fusion
  42.2 3.6 %collective-permute-done.2 = f32[256,128]{1,0:T(8,128)S(1)} collective-permute-done((f32[256,128]{1,0:T(8,128)S(1)}, f32[256,128]{1,0:T(8,128)S(1)}, u32[]{:S(2)}, u32[]{:S(2)}) %collective-permute-start.2) | collective-permute-done | bytes 131104 | tf_op jit(solution)/shard_map/ppermute | solution.py:14
  45.8 2.0 scatter_fusion.1
  48.6 19.4 %reduce-scatter.4.cloned.1.call-done = f32[128,128]{1,0:T(8,128)} async-done(((f32[512,128]{1,0:T(8,128)}), f32[128,128]{1,0:T(8,128)}) %reduce-scatter.4.cloned.1.call-update) | async-done | bytes 65552 | tf_op jit(solution)/shard_map/reduce_scatter | solution.py:97
  68.9 5.8 %all_gather.10 = f32[512,128]{1,0:T(8,128)S(1)} all-gather(f32[128,128]{1,0:T(8,128)S(1)} %multiply_subtract_fusion.5), channel_id=1, replica_groups=mesh['groups'=2,'seg'=4,'bin'=4] {'bin'}, dimensions={0}, use_global_device_ids=true | all-gather | bytes 327680 | tf_op jit(solution)/shard_map/all_gather | solution.py:101
  78.6 3.6 %collective-permute-start.3 = (f32[256,128]{1,0:T(8,128)S(1)}, f32[256,128]{1,0:T(8,128)S(1)}, u32[]{:S(2)}, u32[]{:S(2)}) collective-permute-start(f32[256,128]{1,0:T(8,128)S(1)} %broadcast_multiply_fusion.1), channel_id=1, source_target_pairs={{0,4},{4,8},{8,12},{1,5},{5,9},{9,13},{2,6},{6,10},{10,14},{3,7},{... | collective-permute-start | bytes 393224 | tf_op jit(solution)/shard_map/ppermute | solution.py:14
  88.1 2.0 scatter_fusion.2
  90.2 3.6 %collective-permute-done.4 = f32[256,128]{1,0:T(8,128)S(1)} collective-permute-done((f32[256,128]{1,0:T(8,128)S(1)}, f32[256,128]{1,0:T(8,128)S(1)}, u32[]{:S(2)}, u32[]{:S(2)}) %collective-permute-start.4) | collective-permute-done | bytes 131104 | tf_op jit(solution)/shard_map/ppermute | solution.py:14
  93.7 2.0 scatter_fusion.3
  96.5 19.3 %reduce-scatter.6.cloned.1.call-done = f32[128,128]{1,0:T(8,128)} async-done(((f32[512,128]{1,0:T(8,128)}), f32[128,128]{1,0:T(8,128)}) %reduce-scatter.6.cloned.1.call-update) | async-done | bytes 65552 | tf_op jit(solution)/shard_map/reduce_scatter | solution.py:97
  115.9 1.5 multiply_reduce_fusion.2
  117.4 32.6 %all-reduce.1 = (f32[]{:T(128)}, f32[]{:T(128)}) all-reduce(f32[]{:T(128)} %get-tuple-element.9, f32[]{:T(128)} %get-tuple-element.8), channel_id=1, replica_groups=mesh['groups'=2,'seg'=4,'bin'=4] {'seg','bin'}, use_global_device_ids=true, to_apply=%region_8.0 | all-reduce | flops 2 | bytes 16 | tf_op jit(solution)/shard_map/psum | solution.py:105
  151.4 5.8 %all_gather.11 = f32[512,128]{1,0:T(8,128)S(1)} all-gather(f32[128,128]{1,0:T(8,128)S(1)} %multiply_subtract_fusion.4), channel_id=1, replica_groups=mesh['groups'=2,'seg'=4,'bin'=4] {'bin'}, dimensions={0}, use_global_device_ids=true | all-gather | bytes 327680 | tf_op jit(solution)/shard_map/all_gather | solution.py:101
  166.7 1.5 collective-permute-start.6
  168.6 2.0 scatter_fusion.4
  170.7 3.8 %collective-permute-done.6 = f32[256,128]{1,0:T(8,128)S(1)} collective-permute-done((f32[256,128]{1,0:T(8,128)S(1)}, f32[256,128]{1,0:T(8,128)S(1)}, u32[]{:S(2)}, u32[]{:S(2)}) %collective-permute-start.6) | collective-permute-done | bytes 131104 | tf_op jit(solution)/shard_map/ppermute | solution.py:14
  174.5 2.0 scatter_fusion.5
  177.2 18.7 %reduce-scatter.8.cloned.1.call-done = f32[128,128]{1,0:T(8,128)} async-done(((f32[512,128]{1,0:T(8,128)}), f32[128,128]{1,0:T(8,128)}) %reduce-scatter.8.cloned.1.call-update) | async-done | bytes 65552 | tf_op jit(solution)/shard_map/reduce_scatter | solution.py:97
  195.9 1.6 multiply_reduce_fusion
  197.5 32.7 %all-reduce = (f32[]{:T(128)}, f32[]{:T(128)}) all-reduce(f32[]{:T(128)} %get-tuple-element.7, f32[]{:T(128)} %get-tuple-element.6), channel_id=1, replica_groups=mesh['groups'=2,'seg'=4,'bin'=4] {'seg','bin'}, use_global_device_ids=true, to_apply=%region_15.0 | all-reduce | flops 2 | bytes 16 | tf_op jit(solution)/shard_map/psum | solution.py:105
  (108 shorter events, 39.4 us)
Async XLA Ops:
  7.2 18.9 %copy-start = (bf16[1024,128]{1,0:T(8,128)(2,1)S(1)}, bf16[1024,128]{1,0:T(8,128)(2,1)}, u32[]{:S(2)}) copy-start(bf16[1024,128]{1,0:T(8,128)(2,1)} %param.12) | copy-start | bytes 786436
  7.2 60.8 %reduce-scatter.4.cloned.1.call-start = ((), (), s32[]{:S(2)}) async-start(), calls=%async_computation.3 | async-start | bytes 327680 | tf_op jit(solution)/shard_map/reduce_scatter | solution.py:97
  8.6 11.6 %copy-start.11 = (s32[1,1,2,256]{3,2,1,0:T(2,128)S(1)}, s32[1,1,2,256]{3,2,1,0:T(2,128)}, u32[]{:S(2)}) copy-start(s32[1,1,2,256]{3,2,1,0:T(2,128)} %param.19) | copy-start | bytes 6148
  8.6 28.0 %collective-permute-start = (s32[1]{0:T(128)}, s32[1]{0:T(128)}, u32[]{:S(2)}, u32[]{:S(2)}) collective-permute-start(s32[1]{0:T(128)} %bitcast.23), channel_id=1, source_target_pairs={{0,4},{4,8},{8,12},{1,5},{5,9},{9,13},{2,6},{6,10},{10,14},{3,7},{... | collective-permute-start | bytes 20 | tf_op jit(solution)/shard_map/ppermute | solution.py:14
  21.7 3.0 %copy-start.12 = (s32[1,1,12,2]{2,3,1,0:T(2,128)S(1)}, s32[1,1,12,2]{2,3,1,0:T(2,128)}, u32[]{:S(2)}) copy-start(s32[1,1,12,2]{2,3,1,0:T(2,128)} %param.15) | copy-start | bytes 292
  21.7 16.0 %collective-permute-start.1 = (f32[256,128]{1,0:T(8,128)S(1)}, f32[256,128]{1,0:T(8,128)S(1)}, u32[]{:S(2)}, u32[]{:S(2)}) collective-permute-start(f32[256,128]{1,0:T(8,128)S(1)} %broadcast_multiply_fusion.2), channel_id=1, source_target_pairs={{0,4},{4,8},{8,12},{1,5},{5,9},{9,13},{2,6},{6,10},{10,14},{3,7},{... | collective-permute-start | bytes 393224 | tf_op jit(solution)/shard_map/ppermute | solution.py:14
  26.1 1.0 copy-start.5
  28.5 0.7 copy-start.10
  30.0 0.9 copy-start.4
  34.4 1.0 copy-start.8
  36.6 1.0 copy-start.3
  38.4 7.4 %collective-permute-start.2 = (f32[256,128]{1,0:T(8,128)S(1)}, f32[256,128]{1,0:T(8,128)S(1)}, u32[]{:S(2)}, u32[]{:S(2)}) collective-permute-start(f32[256,128]{1,0:T(8,128)S(1)} %multiply_subtract_fusion.2), channel_id=1, source_target_pairs={{4,0},{8,4},{12,8},{5,1},{9,5},{13,9},{6,2},{10,6},{14,10},{7,3},{... | collective-permute-start | bytes 393224 | tf_op jit(solution)/shard_map/ppermute | solution.py:14
  48.5 19.5 %copy-start.6 = (f32[128,128]{1,0:T(8,128)S(1)}, f32[128,128]{1,0:T(8,128)}, u32[]{:S(2)}) copy-start(f32[128,128]{1,0:T(8,128)} %param.11) | copy-start | bytes 196612
  48.6 67.3 %reduce-scatter.6.cloned.1.call-start = ((), (), s32[]{:S(2)}) async-start(), calls=%async_computation.4 | async-start | bytes 327680 | tf_op jit(solution)/shard_map/reduce_scatter | solution.py:97
  78.6 7.1 %collective-permute-start.3 = (f32[256,128]{1,0:T(8,128)S(1)}, f32[256,128]{1,0:T(8,128)S(1)}, u32[]{:S(2)}, u32[]{:S(2)}) collective-permute-start(f32[256,128]{1,0:T(8,128)S(1)} %broadcast_multiply_fusion.1), channel_id=1, source_target_pairs={{0,4},{4,8},{8,12},{1,5},{5,9},{9,13},{2,6},{6,10},{10,14},{3,7},{... | collective-permute-start | bytes 393224 | tf_op jit(solution)/shard_map/ppermute | solution.py:14
  86.4 7.4 %collective-permute-start.4 = (f32[256,128]{1,0:T(8,128)S(1)}, f32[256,128]{1,0:T(8,128)S(1)}, u32[]{:S(2)}, u32[]{:S(2)}) collective-permute-start(f32[256,128]{1,0:T(8,128)S(1)} %multiply_subtract_fusion.1), channel_id=1, source_target_pairs={{4,0},{8,4},{12,8},{5,1},{9,5},{13,9},{6,2},{10,6},{14,10},{7,3},{... | collective-permute-start | bytes 393224 | tf_op jit(solution)/shard_map/ppermute | solution.py:14
  95.8 0.7 copy-start.2
  96.5 99.4 %reduce-scatter.8.cloned.1.call-start = ((), (), s32[]{:S(2)}) async-start(), calls=%async_computation.5 | async-start | bytes 327680 | tf_op jit(solution)/shard_map/reduce_scatter | solution.py:97
  115.8 35.5 %copy-start.7 = (f32[128,128]{1,0:T(8,128)S(1)}, f32[128,128]{1,0:T(8,128)}, u32[]{:S(2)}) copy-start(f32[128,128]{1,0:T(8,128)} %reduce-scatter.6.cloned.1.call-done) | copy-start | bytes 196612
  161.1 4.8 %collective-permute-start.5 = (f32[256,128]{1,0:T(8,128)S(1)}, f32[256,128]{1,0:T(8,128)S(1)}, u32[]{:S(2)}, u32[]{:S(2)}) collective-permute-start(f32[256,128]{1,0:T(8,128)S(1)} %broadcast_multiply_fusion), channel_id=1, source_target_pairs={{0,4},{4,8},{8,12},{1,5},{5,9},{9,13},{2,6},{6,10},{10,14},{3,7},{... | collective-permute-start | bytes 393224 | tf_op jit(solution)/shard_map/ppermute | solution.py:14
  166.7 7.8 %collective-permute-start.6 = (f32[256,128]{1,0:T(8,128)S(1)}, f32[256,128]{1,0:T(8,128)S(1)}, u32[]{:S(2)}, u32[]{:S(2)}) collective-permute-start(f32[256,128]{1,0:T(8,128)S(1)} %multiply_subtract_fusion), channel_id=1, source_target_pairs={{4,0},{8,4},{12,8},{5,1},{9,5},{13,9},{6,2},{10,6},{14,10},{7,3},{... | collective-permute-start | bytes 393224 | tf_op jit(solution)/shard_map/ppermute | solution.py:14
  176.5 0.7 copy-start.1
  195.9 38.9 %copy-start.9 = (f32[128,128]{1,0:T(8,128)S(1)}, f32[128,128]{1,0:T(8,128)}, u32[]{:S(2)}) copy-start(f32[128,128]{1,0:T(8,128)} %reduce-scatter.8.cloned.1.call-done) | copy-start | bytes 196612
Sparse Core Ops, SparseCore 0:
  48.7 19.2 reduce-scatter.3
  96.6 19.1 reduce-scatter.5
  177.4 18.4 reduce-scatter.7
where the time goes:
time: 243 us; the launch traced here: 242 us
  blocking collectives  82.9 us (34%)
  waiting for transfers between devices  68.4 us (28%)
  between operations  20.9 us (9%)
  other arithmetic  20.5 us (8%)
  starting transfers between devices  17.7 us (7%)
  matrix products  16.7 us (7%)
  local copies, waits for them, and re-layouts  14.9 us (6%)
    psum x2, blocking collectives, fold_sum(): folded = lax.psum((values[0], values[1]), ('seg', 'bin'))  65.3 us
    reduce_scatter x3, waiting for transfers between devices, reduce_rows(): lax.psum_scatter(partial_value, 'bin', scatter_dimension=0, tiled=True)  57.3 us
    ppermute x7, starting transfers between devices, from_behind(): return lax.ppermute(x, axis, pairs)  17.6 us
    scatter-add x6, other arithmetic, apply_local(): return summed.at[rows_low].add(own_term).at[rows_up].add(returned)  12.3 us
    all_gather x2, blocking collectives, spread(): whole_rows = lax.all_gather(vector, 'bin', axis=0, tiled=True)  11.6 us
    ppermute x7, waiting for transfers between devices, from_behind(): return lax.ppermute(x, axis, pairs)  11 us
    all_gather x1, blocking collectives, shards(): start_whole = lax.all_gather(start_factors, 'bin', axis=0, tiled=True)  5.97 us
  transfers between devices with their start and end apart: 10, of which 6 were waited for; matrix products, arithmetic and copies ran while one was open for 11% of the time, Pallas kernels for 0%

commit v1 on v0

--- a/solution.py
+++ b/solution.py
@@ -102,7 +102,7 @@
         return whole_rows
 
     def fold_sum(values):
-        folded = lax.psum((values[0], values[1]), ("seg", "bin"))
+        folded = lax.psum(lax.psum((values[0], values[1]), "bin"), "seg")
         return folded
 
     def image_of(vector):

time: 243 us -> 216 us (0.89)
  blocking collectives: 82.9 us -> 55.4 us
    psum x2 -> x4, blocking collectives: 65.3 us -> 37.8 us  [fold_sum(): folded = lax.psum(lax.psum((values[0], values[1]), 'bin'), 'seg')]
  transfers between devices with their start and end apart: 10 -> 10, of which waited for: 6 -> 6; matrix products, arithmetic and copies ran while one was open for 11% -> 12% of each run, Pallas kernels for 0% -> 0%
where the time goes in v1:
time: 216 us; the launch traced here: 215 us
  waiting for transfers between devices  68.8 us (32%)
  blocking collectives  55.4 us (26%)
  between operations  20.9 us (10%)
  other arithmetic  20.4 us (9%)
  starting transfers between devices  17.7 us (8%)
  matrix products  16.7 us (8%)
  local copies, waits for them, and re-layouts  14.9 us (7%)
    reduce_scatter x3, waiting for transfers between devices, reduce_rows(): lax.psum_scatter(partial_value, 'bin', scatter_dimension=0, tiled=True)  57.7 us
    psum x4, blocking collectives, fold_sum(): folded = lax.psum(lax.psum((values[0], values[1]), 'bin'), 'seg')  37.8 us
    ppermute x7, starting transfers between devices, from_behind(): return lax.ppermute(x, axis, pairs)  17.6 us
    scatter-add x6, other arithmetic, apply_local(): return summed.at[rows_low].add(own_term).at[rows_up].add(returned)  12.3 us
    all_gather x2, blocking collectives, spread(): whole_rows = lax.all_gather(vector, 'bin', axis=0, tiled=True)  11.6 us
    ppermute x7, waiting for transfers between devices, from_behind(): return lax.ppermute(x, axis, pairs)  11 us
    all_gather x1, blocking collectives, shards(): start_whole = lax.all_gather(start_factors, 'bin', axis=0, tiled=True)  5.97 us
  transfers between devices with their start and end apart: 10, of which 6 were waited for; matrix products, arithmetic and copies ran while one was open for 12% of the time, Pallas kernels for 0%

profile of v1, /device:TPU:0, one launch (start us, length us, event | category | flops | bytes accessed | tf_op | source)
XLA Modules:
  0.0 214.8 jit_solution(9673407274142111884)
XLA Ops:
  8.6 5.6 %collective-permute-start = (s32[1]{0:T(128)}, s32[1]{0:T(128)}, u32[]{:S(2)}, u32[]{:S(2)}) collective-permute-start(s32[1]{0:T(128)} %bitcast.23), channel_id=1, source_target_pairs={{0,4},{4,8},{8,12},{1,5},{5,9},{9,13},{2,6},{6,10},{10,14},{3,7},{... | collective-permute-start | bytes 20 | tf_op jit(solution)/shard_map/ppermute | solution.py:14
  14.2 6.0 %all_gather.9 = f32[512,128]{1,0:T(8,128)S(1)} all-gather(f32[128,128]{1,0:T(8,128)} %param.11), channel_id=1, replica_groups=mesh['groups'=2,'seg'=4,'bin'=4] {'bin'}, dimensions={0}, use_global_device_ids=true | all-gather | bytes 327680 | tf_op jit(solution)/shard_map/all_gather | solution.py:111
  21.7 3.0 %collective-permute-start.1 = (f32[256,128]{1,0:T(8,128)S(1)}, f32[256,128]{1,0:T(8,128)S(1)}, u32[]{:S(2)}, u32[]{:S(2)}) collective-permute-start(f32[256,128]{1,0:T(8,128)S(1)} %broadcast_multiply_fusion.2), channel_id=1, source_target_pairs={{0,4},{4,8},{8,12},{1,5},{5,9},{9,13},{2,6},{6,10},{10,14},{3,7},{... | collective-permute-start | bytes 393224 | tf_op jit(solution)/shard_map/ppermute | solution.py:14
  40.1 2.0 scatter_fusion
  42.2 3.6 %collective-permute-done.2 = f32[256,128]{1,0:T(8,128)S(1)} collective-permute-done((f32[256,128]{1,0:T(8,128)S(1)}, f32[256,128]{1,0:T(8,128)S(1)}, u32[]{:S(2)}, u32[]{:S(2)}) %collective-permute-start.2) | collective-permute-done | bytes 131104 | tf_op jit(solution)/shard_map/ppermute | solution.py:14
  45.8 2.0 scatter_fusion.1
  48.6 19.4 %reduce-scatter.4.cloned.1.call-done = f32[128,128]{1,0:T(8,128)} async-done(((f32[512,128]{1,0:T(8,128)}), f32[128,128]{1,0:T(8,128)}) %reduce-scatter.4.cloned.1.call-update) | async-done | bytes 65552 | tf_op jit(solution)/shard_map/reduce_scatter | solution.py:97
  68.9 5.8 %all_gather.10 = f32[512,128]{1,0:T(8,128)S(1)} all-gather(f32[128,128]{1,0:T(8,128)S(1)} %multiply_subtract_fusion.5), channel_id=1, replica_groups=mesh['groups'=2,'seg'=4,'bin'=4] {'bin'}, dimensions={0}, use_global_device_ids=true | all-gather | bytes 327680 | tf_op jit(solution)/shard_map/all_gather | solution.py:101
  78.6 3.6 %collective-permute-start.3 = (f32[256,128]{1,0:T(8,128)S(1)}, f32[256,128]{1,0:T(8,128)S(1)}, u32[]{:S(2)}, u32[]{:S(2)}) collective-permute-start(f32[256,128]{1,0:T(8,128)S(1)} %broadcast_multiply_fusion.1), channel_id=1, source_target_pairs={{0,4},{4,8},{8,12},{1,5},{5,9},{9,13},{2,6},{6,10},{10,14},{3,7},{... | collective-permute-start | bytes 393224 | tf_op jit(solution)/shard_map/ppermute | solution.py:14
  88.1 2.0 scatter_fusion.2
  90.2 3.6 %collective-permute-done.4 = f32[256,128]{1,0:T(8,128)S(1)} collective-permute-done((f32[256,128]{1,0:T(8,128)S(1)}, f32[256,128]{1,0:T(8,128)S(1)}, u32[]{:S(2)}, u32[]{:S(2)}) %collective-permute-start.4) | collective-permute-done | bytes 131104 | tf_op jit(solution)/shard_map/ppermute | solution.py:14
  93.7 2.0 scatter_fusion.3
  96.5 19.3 %reduce-scatter.6.cloned.1.call-done = f32[128,128]{1,0:T(8,128)} async-done(((f32[512,128]{1,0:T(8,128)}), f32[128,128]{1,0:T(8,128)}) %reduce-scatter.6.cloned.1.call-update) | async-done | bytes 65552 | tf_op jit(solution)/shard_map/reduce_scatter | solution.py:97
  115.9 1.5 multiply_reduce_fusion.2
  117.4 6.4 %all-reduce.1 = (f32[]{:T(128)}, f32[]{:T(128)}) all-reduce(f32[]{:T(128)} %get-tuple-element.9, f32[]{:T(128)} %get-tuple-element.8), channel_id=1, replica_groups=mesh['groups'=2,'seg'=4,'bin'=4] {'bin'}, use_global_device_ids=true, to_apply=%region_8.0 | all-reduce | flops 2 | bytes 16 | tf_op jit(solution)/shard_map/psum | solution.py:105
  123.8 12.5 %all-reduce.3 = (f32[]{:T(128)}, f32[]{:T(128)}) all-reduce(f32[]{:T(128)} %get-tuple-element.16, f32[]{:T(128)} %get-tuple-element.17), channel_id=1, replica_groups=mesh['groups'=2,'seg'=4,'bin'=4] {'seg'}, use_global_device_ids=true, to_apply=%region_9.0 | all-reduce | flops 2 | bytes 16 | tf_op jit(solution)/shard_map/psum | solution.py:105
  137.6 5.8 %all_gather.11 = f32[512,128]{1,0:T(8,128)S(1)} all-gather(f32[128,128]{1,0:T(8,128)S(1)} %multiply_subtract_fusion.4), channel_id=1, replica_groups=mesh['groups'=2,'seg'=4,'bin'=4] {'bin'}, dimensions={0}, use_global_device_ids=true | all-gather | bytes 327680 | tf_op jit(solution)/shard_map/all_gather | solution.py:101
  154.8 2.0 scatter_fusion.4
  156.9 3.8 %collective-permute-done.6 = f32[256,128]{1,0:T(8,128)S(1)} collective-permute-done((f32[256,128]{1,0:T(8,128)S(1)}, f32[256,128]{1,0:T(8,128)S(1)}, u32[]{:S(2)}, u32[]{:S(2)}) %collective-permute-start.6) | collective-permute-done | bytes 131104 | tf_op jit(solution)/shard_map/ppermute | solution.py:14
  160.7 2.0 scatter_fusion.5
  163.4 19.0 %reduce-scatter.8.cloned.1.call-done = f32[128,128]{1,0:T(8,128)} async-done(((f32[512,128]{1,0:T(8,128)}), f32[128,128]{1,0:T(8,128)}) %reduce-scatter.8.cloned.1.call-update) | async-done | bytes 65552 | tf_op jit(solution)/shard_map/reduce_scatter | solution.py:97
  182.5 1.6 multiply_reduce_fusion
  184.1 6.4 %all-reduce = (f32[]{:T(128)}, f32[]{:T(128)}) all-reduce(f32[]{:T(128)} %get-tuple-element.7, f32[]{:T(128)} %get-tuple-element.6), channel_id=1, replica_groups=mesh['groups'=2,'seg'=4,'bin'=4] {'bin'}, use_global_device_ids=true, to_apply=%region_17.0 | all-reduce | flops 2 | bytes 16 | tf_op jit(solution)/shard_map/psum | solution.py:105
  190.5 12.5 %all-reduce.2 = (f32[]{:T(128)}, f32[]{:T(128)}) all-reduce(f32[]{:T(128)} %get-tuple-element.14, f32[]{:T(128)} %get-tuple-element.15), channel_id=1, replica_groups=mesh['groups'=2,'seg'=4,'bin'=4] {'seg'}, use_global_device_ids=true, to_apply=%region_18.0 | all-reduce | flops 2 | bytes 16 | tf_op jit(solution)/shard_map/psum | solution.py:105
  (110 shorter events, 42.3 us)
Async XLA Ops:
  7.2 18.9 %copy-start = (bf16[1024,128]{1,0:T(8,128)(2,1)S(1)}, bf16[1024,128]{1,0:T(8,128)(2,1)}, u32[]{:S(2)}) copy-start(bf16[1024,128]{1,0:T(8,128)(2,1)} %param.12) | copy-start | bytes 786436
  7.2 60.8 %reduce-scatter.4.cloned.1.call-start = ((), (), s32[]{:S(2)}) async-start(), calls=%async_computation.3 | async-start | bytes 327680 | tf_op jit(solution)/shard_map/reduce_scatter | solution.py:97
  8.6 11.6 %copy-start.11 = (s32[1,1,2,256]{3,2,1,0:T(2,128)S(1)}, s32[1,1,2,256]{3,2,1,0:T(2,128)}, u32[]{:S(2)}) copy-start(s32[1,1,2,256]{3,2,1,0:T(2,128)} %param.19) | copy-start | bytes 6148
  8.6 28.0 %collective-permute-start = (s32[1]{0:T(128)}, s32[1]{0:T(128)}, u32[]{:S(2)}, u32[]{:S(2)}) collective-permute-start(s32[1]{0:T(128)} %bitcast.23), channel_id=1, source_target_pairs={{0,4},{4,8},{8,12},{1,5},{5,9},{9,13},{2,6},{6,10},{10,14},{3,7},{... | collective-permute-start | bytes 20 | tf_op jit(solution)/shard_map/ppermute | solution.py:14
  21.7 3.0 %copy-start.12 = (s32[1,1,12,2]{2,3,1,0:T(2,128)S(1)}, s32[1,1,12,2]{2,3,1,0:T(2,128)}, u32[]{:S(2)}) copy-start(s32[1,1,12,2]{2,3,1,0:T(2,128)} %param.15) | copy-start | bytes 292
  21.7 16.0 %collective-permute-start.1 = (f32[256,128]{1,0:T(8,128)S(1)}, f32[256,128]{1,0:T(8,128)S(1)}, u32[]{:S(2)}, u32[]{:S(2)}) collective-permute-start(f32[256,128]{1,0:T(8,128)S(1)} %broadcast_multiply_fusion.2), channel_id=1, source_target_pairs={{0,4},{4,8},{8,12},{1,5},{5,9},{9,13},{2,6},{6,10},{10,14},{3,7},{... | collective-permute-start | bytes 393224 | tf_op jit(solution)/shard_map/ppermute | solution.py:14
  26.1 1.0 copy-start.5
  28.5 0.7 copy-start.10
  30.0 0.9 copy-start.4
  34.4 1.0 copy-start.8
  36.6 1.0 copy-start.3
  38.4 7.4 %collective-permute-start.2 = (f32[256,128]{1,0:T(8,128)S(1)}, f32[256,128]{1,0:T(8,128)S(1)}, u32[]{:S(2)}, u32[]{:S(2)}) collective-permute-start(f32[256,128]{1,0:T(8,128)S(1)} %multiply_subtract_fusion.2), channel_id=1, source_target_pairs={{4,0},{8,4},{12,8},{5,1},{9,5},{13,9},{6,2},{10,6},{14,10},{7,3},{... | collective-permute-start | bytes 393224 | tf_op jit(solution)/shard_map/ppermute | solution.py:14
  48.5 19.5 %copy-start.6 = (f32[128,128]{1,0:T(8,128)S(1)}, f32[128,128]{1,0:T(8,128)}, u32[]{:S(2)}) copy-start(f32[128,128]{1,0:T(8,128)} %param.11) | copy-start | bytes 196612
  48.6 67.3 %reduce-scatter.6.cloned.1.call-start = ((), (), s32[]{:S(2)}) async-start(), calls=%async_computation.4 | async-start | bytes 327680 | tf_op jit(solution)/shard_map/reduce_scatter | solution.py:97
  78.6 7.1 %collective-permute-start.3 = (f32[256,128]{1,0:T(8,128)S(1)}, f32[256,128]{1,0:T(8,128)S(1)}, u32[]{:S(2)}, u32[]{:S(2)}) collective-permute-start(f32[256,128]{1,0:T(8,128)S(1)} %broadcast_multiply_fusion.1), channel_id=1, source_target_pairs={{0,4},{4,8},{8,12},{1,5},{5,9},{9,13},{2,6},{6,10},{10,14},{3,7},{... | collective-permute-start | bytes 393224 | tf_op jit(solution)/shard_map/ppermute | solution.py:14
  86.4 7.4 %collective-permute-start.4 = (f32[256,128]{1,0:T(8,128)S(1)}, f32[256,128]{1,0:T(8,128)S(1)}, u32[]{:S(2)}, u32[]{:S(2)}) collective-permute-start(f32[256,128]{1,0:T(8,128)S(1)} %multiply_subtract_fusion.1), channel_id=1, source_target_pairs={{4,0},{8,4},{12,8},{5,1},{9,5},{13,9},{6,2},{10,6},{14,10},{7,3},{... | collective-permute-start | bytes 393224 | tf_op jit(solution)/shard_map/ppermute | solution.py:14
  95.8 0.7 copy-start.2
  96.5 86.0 %reduce-scatter.8.cloned.1.call-start = ((), (), s32[]{:S(2)}) async-start(), calls=%async_computation.5 | async-start | bytes 327680 | tf_op jit(solution)/shard_map/reduce_scatter | solution.py:97
  115.8 21.7 %copy-start.7 = (f32[128,128]{1,0:T(8,128)S(1)}, f32[128,128]{1,0:T(8,128)}, u32[]{:S(2)}) copy-start(f32[128,128]{1,0:T(8,128)} %reduce-scatter.6.cloned.1.call-done) | copy-start | bytes 196612
  147.4 4.8 %collective-permute-start.5 = (f32[256,128]{1,0:T(8,128)S(1)}, f32[256,128]{1,0:T(8,128)S(1)}, u32[]{:S(2)}, u32[]{:S(2)}) collective-permute-start(f32[256,128]{1,0:T(8,128)S(1)} %broadcast_multiply_fusion), channel_id=1, source_target_pairs={{0,4},{4,8},{8,12},{1,5},{5,9},{9,13},{2,6},{6,10},{10,14},{3,7},{... | collective-permute-start | bytes 393224 | tf_op jit(solution)/shard_map/ppermute | solution.py:14
  152.9 7.8 %collective-permute-start.6 = (f32[256,128]{1,0:T(8,128)S(1)}, f32[256,128]{1,0:T(8,128)S(1)}, u32[]{:S(2)}, u32[]{:S(2)}) collective-permute-start(f32[256,128]{1,0:T(8,128)S(1)} %multiply_subtract_fusion), channel_id=1, source_target_pairs={{4,0},{8,4},{12,8},{5,1},{9,5},{13,9},{6,2},{10,6},{14,10},{7,3},{... | collective-permute-start | bytes 393224 | tf_op jit(solution)/shard_map/ppermute | solution.py:14
  162.7 0.7 copy-start.1
  182.5 25.2 %copy-start.9 = (f32[128,128]{1,0:T(8,128)S(1)}, f32[128,128]{1,0:T(8,128)}, u32[]{:S(2)}) copy-start(f32[128,128]{1,0:T(8,128)} %reduce-scatter.8.cloned.1.call-done) | copy-start | bytes 196612
Sparse Core Ops, SparseCore 0:
  48.7 19.2 reduce-scatter.3
  96.6 19.1 reduce-scatter.5
  163.6 18.8 reduce-scatter.7
